TPU v7x, 32 devices: a whole 2x2x4 slice. The times are simulated.
32 devices in a mesh: rows: 2 (over x), cols: 4 (over z), slabs: 2 (over y), trial: 2 (over core).
Axes of the slice: x: 2, y: 2, z: 4, core: 2. Of those that a mesh axis runs over, the one named last changes fastest.
Arguments:
- field_values: float32 [32, 64, 128, 128], P(('trial', 'rows'), 'cols', 'slabs'), parts along dimension 0, may hold values from 0.2 to 1.8
- crowding: float32 [32, 64, 128, 128], P(('trial', 'rows'), 'cols', 'slabs'), parts along dimension 0, may hold values from 0.5 to 2
Outputs:
- potential: float32 [32, 64, 128, 128], P(('trial', 'rows'), 'cols', 'slabs'), parts along dimension 0
- field_values_end: float32 [32, 64, 128, 128], P(('trial', 'rows'), 'cols', 'slabs'), parts along dimension 0
There are 2 independent parts, one for each index of `trial`. A program takes and returns all parts, laid end to end along the dimension named above; each array names one. Nothing has to cross between parts.
All inputs are finite; a program needn't handle non-finite values.
Results may differ from a plain program's by a relative error of at most 0.00002.
Values sent between devices are 32-bit elements; how exact they have to be, the bound alone decides.
A program may use at most 64 MiB of HBM per device.

v0:
```python
import jax
import jax.numpy as jnp
from jax import lax
from jax.sharding import PartitionSpec as P

STEPS = 3


def padded_2(shard, sides, width):
    for axis, dim in sides:
        devices, length = (lax.axis_size(axis), shard.shape[dim])
        up = [(i, (i + 1) % devices) for i in range(devices - 1)]
        down = [(j, i) for i, j in up]
        last = lax.slice_in_dim(shard, length - width, length, axis=dim)
        initial = lax.slice_in_dim(shard, 0, width, axis=dim)
        before = lax.ppermute(last, axis, up)
        after = lax.ppermute(initial, axis, down)
        shard = jnp.concatenate([before, shard, after], axis=dim)
    return shard


def entering(part, axis, combine, identity):
    place = lax.axis_index(axis)
    gathered = lax.all_gather(part, axis)
    state = jnp.zeros_like(part) + jnp.asarray(identity, part.dtype)

    def one(lap, state):
        return combine(state, lax.dynamic_index_in_dim(gathered, lap, 0, False))

    return lax.fori_loop(0, place, one, state)


def without_rim(values, dims):
    for dim in dims:
        values = lax.slice_in_dim(values, 1, values.shape[dim] - 1, axis=dim)
    return values


def shifted_cells(values, dim, start, dims):
    others = [other for other in dims if other != dim]
    values = without_rim(values, others)
    return lax.slice_in_dim(values, start, start + values.shape[dim] - 2, axis=dim)


def march_step(padded, crowding):
    middle = without_rim(padded, (0, 1, 2))
    lower = [shifted_cells(padded, dim, 0, (0, 1, 2)) for dim in (0, 1, 2)]
    upper = [shifted_cells(padded, dim, 2, (0, 1, 2)) for dim in (0, 1, 2)]
    spread = lower[0] + upper[0] + lower[1] + upper[1] + lower[2] + upper[2] - 6.0 * middle
    return middle + 0.1 * spread + 0.2 * middle * (1.0 - middle * crowding)


def on_device(field_values, crowding):
    for step in range(STEPS):
        padded = padded_2(field_values, (("rows", 0), ("cols", 1), ("slabs", 2)), 1)
        field_values = march_step(padded, crowding)
    here = jnp.cumsum(field_values, axis=0)
    total = lax.slice_in_dim(here, here.shape[0] - 1, here.shape[0], axis=0)

    def add_pair(earlier_total, later_total):
        return earlier_total + later_total

    below = entering(total, "rows", add_pair, jnp.zeros_like(total))
    potential = (here + below) / (field_values.shape[0] * lax.axis_size("rows"))
    return (potential, field_values)


def solution(mesh):
    in_specs = (
        P(("trial", "rows"), "cols", "slabs", None),
        P(("trial", "rows"), "cols", "slabs", None),
    )
    out_specs = (
        P(("trial", "rows"), "cols", "slabs", None),
        P(("trial", "rows"), "cols", "slabs", None),
    )
    return jax.shard_map(
        on_device, mesh=mesh, in_specs=in_specs, out_specs=out_specs, check_vma=False
    )
```

profile of v0, /device:TPU:0, one launch (start us, length us, event | category | flops | bytes accessed | tf_op | source)
XLA Modules:
  0.0 182.9 jit_solution(2595272963306853123)
XLA Ops:
  7.2 0.0 all-gather.3.cloned.1.call-start
  7.2 1.3 fusion.30
  8.5 4.9 %collective-permute-start = (f32[1,16,64,128]{3,2,1,0:T(8,128)S(1)}, f32[1,16,64,128]{3,2,1,0:T(8,128)S(1)}, u32[]{:S(2)}, u32[]{:S(2)}) collective-permute-start(f32[1,16,64,128]{3,2,1,0:T(8,128)S(1)} %get-tuple-element.65), channel_id=1, source_target_pairs={{0,16},{1,17},{2,18},{3,19},{4,20},{5,21},{6,22},{7,23},{8,24},{9,... | collective-permute-start | bytes 1572872 | tf_op jit(solution)/shard_map/ppermute | solution.py:16
  13.4 1.3 collective-permute-start.1
  14.7 9.8 %collective-permute-done = f32[1,16,64,128]{3,2,1,0:T(8,128)S(1)} collective-permute-done((f32[1,16,64,128]{3,2,1,0:T(8,128)S(1)}, f32[1,16,64,128]{3,2,1,0:T(8,128)S(1)}, u32[]{:S(2)}, u32[]{:S(2)}) %collective-permute-start) | collective-permute-done | bytes 524320 | tf_op jit(solution)/shard_map/ppermute | solution.py:16
  24.6 2.5 %constant_dynamic-update-slice_fusion.1 = f32[10,16,64,128]{3,2,1,0:T(8,128)S(1)} fusion(f32[10,16,64,128]{3,2,1,0:T(8,128)S(1)} %constant_dynamic-update-slice_fusion.2, f32[8,16,64,128]{3,2,1,0:T(8,128)} %param.4), kind=kLoop, calls=%fused_computation.95 | loop fusion | bytes 8388608
  27.1 1.6 collective-permute-done.1
  28.7 0.0 copy-start
  28.8 0.1 fusion.27
  28.8 3.8 %collective-permute-start.2 = (f32[10,1,64,128]{3,2,1,0:T(8,128)S(1)}, f32[10,1,64,128]{3,2,1,0:T(8,128)S(1)}, u32[]{:S(2)}, u32[]{:S(2)}) collective-permute-start(f32[10,1,64,128]{3,2,1,0:T(8,128)S(1)} %get-tuple-element.58), channel_id=1, source_target_pairs={{0,4},{4,8},{8,12},{1,5},{5,9},{9,13},{2,6},{6,10},{10,14},{3,7},{... | collective-permute-start | bytes 983048 | tf_op jit(solution)/shard_map/ppermute | solution.py:16
  32.6 1.3 collective-permute-start.3
  33.9 4.5 %collective-permute-done.2 = f32[10,1,64,128]{3,2,1,0:T(8,128)S(1)} collective-permute-done((f32[10,1,64,128]{3,2,1,0:T(8,128)S(1)}, f32[10,1,64,128]{3,2,1,0:T(8,128)S(1)}, u32[]{:S(2)}, u32[]{:S(2)}) %collective-permute-start.2) | collective-permute-done | bytes 327712 | tf_op jit(solution)/shard_map/ppermute | solution.py:16
  38.4 4.1 %collective-permute-done.3 = f32[10,1,64,128]{3,2,1,0:T(8,128)S(1)} collective-permute-done((f32[10,1,64,128]{3,2,1,0:T(8,128)S(1)}, f32[10,1,64,128]{3,2,1,0:T(8,128)S(1)}, u32[]{:S(2)}, u32[]{:S(2)}) %collective-permute-start.3) | collective-permute-done | bytes 327712 | tf_op jit(solution)/shard_map/ppermute | solution.py:17
  42.5 0.1 pad_maximum_fusion.64
  42.7 3.4 %collective-permute-start.4 = (f32[10,18,1,128]{3,1,2,0:T(8,128)S(1)}, f32[10,18,1,128]{3,1,2,0:T(8,128)S(1)}, u32[]{:S(2)}, u32[]{:S(2)}) collective-permute-start(f32[10,18,1,128]{3,1,2,0:T(8,128)S(1)} %copy.22), channel_id=1, source_target_pairs={{0,2},{1,3},{4,6},{5,7},{8,10},{9,11},{12,14},{13,15},{16,18},{17,... | collective-permute-start | bytes 276488 | tf_op jit(solution)/shard_map/ppermute | solution.py:16
  46.1 1.3 collective-permute-start.5
  47.4 1.1 collective-permute-done.4
  48.5 0.1 copy.23
  48.6 4.3 %collective-permute-done.5 = f32[10,18,1,128]{3,1,2,0:T(8,128)S(1)} collective-permute-done((f32[10,18,1,128]{3,1,2,0:T(8,128)S(1)}, f32[10,18,1,128]{3,1,2,0:T(8,128)S(1)}, u32[]{:S(2)}, u32[]{:S(2)}) %collective-permute-start.5) | collective-permute-done | bytes 92192 | tf_op jit(solution)/shard_map/ppermute | solution.py:17
  52.9 0.0 copy-done.2
  52.9 0.7 copy.25
  53.6 8.3 %fusion.22 = f32[8,16,64,128]{3,2,1,0:T(8,128)S(1)} fusion(f32[8,16,64,128]{3,2,1,0:T(8,128)} %param.4, f32[10,18,1,128]{3,2,1,0:T(1,128)} %copy.25, f32[10,1,64,128]{3,2,1,0:T(8,128)} %copy-done.3, f32[10,16,64,128]{3,2,1,0:T(8,128)S(1)} %constant_dynamic-update-slice_fusion, f32[10,1,64,128]{3,2,1,0:T(8,128)S(1)} %collective-permute-done.2, ...), kind=kLoop, calls=%fused_computation.60 | loop fusion | flops 25165824 | bytes 19714048 | tf_op jit(solution)/shard_map/add | solution.py:50
  62.0 0.1 fusion.29
  62.1 3.1 %collective-permute-start.6 = (f32[1,16,64,128]{3,2,1,0:T(8,128)S(1)}, f32[1,16,64,128]{3,2,1,0:T(8,128)S(1)}, u32[]{:S(2)}, u32[]{:S(2)}) collective-permute-start(f32[1,16,64,128]{3,2,1,0:T(8,128)S(1)} %get-tuple-element.62), channel_id=1, source_target_pairs={{0,16},{1,17},{2,18},{3,19},{4,20},{5,21},{6,22},{7,23},{8,24},{9,... | collective-permute-start | bytes 1572872 | tf_op jit(solution)/shard_map/ppermute | solution.py:16
  65.2 1.3 collective-permute-start.7
  66.5 6.4 %collective-permute-done.6 = f32[1,16,64,128]{3,2,1,0:T(8,128)S(1)} collective-permute-done((f32[1,16,64,128]{3,2,1,0:T(8,128)S(1)}, f32[1,16,64,128]{3,2,1,0:T(8,128)S(1)}, u32[]{:S(2)}, u32[]{:S(2)}) %collective-permute-start.6) | collective-permute-done | bytes 524320 | tf_op jit(solution)/shard_map/ppermute | solution.py:16
  72.9 4.1 %collective-permute-done.7 = f32[1,16,64,128]{3,2,1,0:T(8,128)S(1)} collective-permute-done((f32[1,16,64,128]{3,2,1,0:T(8,128)S(1)}, f32[1,16,64,128]{3,2,1,0:T(8,128)S(1)}, u32[]{:S(2)}, u32[]{:S(2)}) %collective-permute-start.7) | collective-permute-done | bytes 524320 | tf_op jit(solution)/shard_map/ppermute | solution.py:17
  77.1 3.5 %collective-permute-start.8 = (f32[10,1,64,128]{3,2,1,0:T(8,128)S(1)}, f32[10,1,64,128]{3,2,1,0:T(8,128)S(1)}, u32[]{:S(2)}, u32[]{:S(2)}) collective-permute-start(f32[10,1,64,128]{3,2,1,0:T(8,128)S(1)} %get-tuple-element.56), channel_id=1, source_target_pairs={{0,4},{4,8},{8,12},{1,5},{5,9},{9,13},{2,6},{6,10},{10,14},{3,7},{... | collective-permute-start | bytes 983048 | tf_op jit(solution)/shard_map/ppermute | solution.py:16
  80.6 1.3 collective-permute-start.9
  81.9 3.3 %collective-permute-done.8 = f32[10,1,64,128]{3,2,1,0:T(8,128)S(1)} collective-permute-done((f32[10,1,64,128]{3,2,1,0:T(8,128)S(1)}, f32[10,1,64,128]{3,2,1,0:T(8,128)S(1)}, u32[]{:S(2)}, u32[]{:S(2)}) %collective-permute-start.8) | collective-permute-done | bytes 327712 | tf_op jit(solution)/shard_map/ppermute | solution.py:16
  85.1 4.4 %collective-permute-done.9 = f32[10,1,64,128]{3,2,1,0:T(8,128)S(1)} collective-permute-done((f32[10,1,64,128]{3,2,1,0:T(8,128)S(1)}, f32[10,1,64,128]{3,2,1,0:T(8,128)S(1)}, u32[]{:S(2)}, u32[]{:S(2)}) %collective-permute-start.9) | collective-permute-done | bytes 327712 | tf_op jit(solution)/shard_map/ppermute | solution.py:17
  89.6 0.1 pad_maximum_fusion.61
  89.7 1.8 collective-permute-start.10
  91.5 1.3 collective-permute-start.11
  92.8 1.1 collective-permute-done.10
  93.9 0.1 copy.27
  94.0 4.3 %collective-permute-done.11 = f32[10,18,1,128]{3,1,2,0:T(8,128)S(1)} collective-permute-done((f32[10,18,1,128]{3,1,2,0:T(8,128)S(1)}, f32[10,18,1,128]{3,1,2,0:T(8,128)S(1)}, u32[]{:S(2)}, u32[]{:S(2)}) %collective-permute-start.11) | collective-permute-done | bytes 92192 | tf_op jit(solution)/shard_map/ppermute | solution.py:17
  98.3 0.1 copy.29
  98.4 7.9 %fusion.13 = f32[8,16,64,128]{3,2,1,0:T(8,128)S(1)} fusion(f32[8,16,64,128]{3,2,1,0:T(8,128)S(1)} %fusion.22, f32[10,18,1,128]{3,2,1,0:T(1,128)S(1)} %copy.29, f32[10,1,64,128]{3,2,1,0:T(8,128)S(1)} %collective-permute-done.9, f32[10,1,64,128]{3,2,1,0:T(8,128)S(1)} %collective-permute-done.8, f32[1,16,64,128]{3,2,1,0:T(8,128)S(1)} %collective-permute-done.7, ...), kind=kLoop, calls=%fused_computation.33 | loop fusion | flops 33554432 | bytes 14471168 | tf_op jit(solution)/shard_map/add | solution.py:50
  106.3 0.1 fusion.28
  106.4 1.5 collective-permute-start.12
  107.9 1.3 collective-permute-start.13
  109.2 5.3 %collective-permute-done.12 = f32[1,16,64,128]{3,2,1,0:T(8,128)S(1)} collective-permute-done((f32[1,16,64,128]{3,2,1,0:T(8,128)S(1)}, f32[1,16,64,128]{3,2,1,0:T(8,128)S(1)}, u32[]{:S(2)}, u32[]{:S(2)}) %collective-permute-start.12) | collective-permute-done | bytes 524320 | tf_op jit(solution)/shard_map/ppermute | solution.py:16
  114.6 4.4 %collective-permute-done.13 = f32[1,16,64,128]{3,2,1,0:T(8,128)S(1)} collective-permute-done((f32[1,16,64,128]{3,2,1,0:T(8,128)S(1)}, f32[1,16,64,128]{3,2,1,0:T(8,128)S(1)}, u32[]{:S(2)}, u32[]{:S(2)}) %collective-permute-start.13) | collective-permute-done | bytes 524320 | tf_op jit(solution)/shard_map/ppermute | solution.py:17
  119.0 0.1 pad_maximum_fusion.48
  119.1 3.5 %collective-permute-start.14 = (f32[10,1,64,128]{3,2,1,0:T(8,128)S(1)}, f32[10,1,64,128]{3,2,1,0:T(8,128)S(1)}, u32[]{:S(2)}, u32[]{:S(2)}) collective-permute-start(f32[10,1,64,128]{3,2,1,0:T(8,128)S(1)} %get-tuple-element.54), channel_id=1, source_target_pairs={{0,4},{4,8},{8,12},{1,5},{5,9},{9,13},{2,6},{6,10},{10,14},{3,7},{... | collective-permute-start | bytes 983048 | tf_op jit(solution)/shard_map/ppermute | solution.py:16
  122.6 1.3 collective-permute-start.15
  123.9 3.3 %collective-permute-done.14 = f32[10,1,64,128]{3,2,1,0:T(8,128)S(1)} collective-permute-done((f32[10,1,64,128]{3,2,1,0:T(8,128)S(1)}, f32[10,1,64,128]{3,2,1,0:T(8,128)S(1)}, u32[]{:S(2)}, u32[]{:S(2)}) %collective-permute-start.14) | collective-permute-done | bytes 327712 | tf_op jit(solution)/shard_map/ppermute | solution.py:16
  127.1 4.4 %collective-permute-done.15 = f32[10,1,64,128]{3,2,1,0:T(8,128)S(1)} collective-permute-done((f32[10,1,64,128]{3,2,1,0:T(8,128)S(1)}, f32[10,1,64,128]{3,2,1,0:T(8,128)S(1)}, u32[]{:S(2)}, u32[]{:S(2)}) %collective-permute-start.15) | collective-permute-done | bytes 327712 | tf_op jit(solution)/shard_map/ppermute | solution.py:17
  131.5 0.1 pad_maximum_fusion.56
  131.7 1.5 collective-permute-start.16
  133.2 1.3 collective-permute-start.17
  134.5 1.1 collective-permute-done.16
  135.6 0.1 copy.31
  135.7 4.3 %collective-permute-done.17 = f32[10,18,1,128]{3,1,2,0:T(8,128)S(1)} collective-permute-done((f32[10,18,1,128]{3,1,2,0:T(8,128)S(1)}, f32[10,18,1,128]{3,1,2,0:T(8,128)S(1)}, u32[]{:S(2)}, u32[]{:S(2)}) %collective-permute-start.17) | collective-permute-done | bytes 92192 | tf_op jit(solution)/shard_map/ppermute | solution.py:17
  140.0 0.1 copy.33
  140.1 8.2 %fusion.4 = f32[8,16,64,128]{3,2,1,0:T(8,128)S(1)} fusion(f32[8,16,64,128]{3,2,1,0:T(8,128)S(1)} %fusion.13, f32[10,18,1,128]{3,2,1,0:T(1,128)S(1)} %copy.33, f32[10,1,64,128]{3,2,1,0:T(8,128)S(1)} %collective-permute-done.15, f32[10,1,64,128]{3,2,1,0:T(8,128)S(1)} %collective-permute-done.14, f32[1,16,64,128]{3,2,1,0:T(8,128)S(1)} %collective-permute-done.13, ...), kind=kLoop, calls=%fused_computation.6 | loop fusion | flops 33554432 | bytes 14471168 | tf_op jit(solution)/shard_map/add | solution.py:50
  148.3 0.0 copy-start.1
  148.3 2.7 %fusion.31 = f32[8,16,64,128]{3,2,1,0:T(8,128)} fusion(f32[8,16,64,128]{3,2,1,0:T(8,128)S(1)} %fusion.4), kind=kOutput, calls=%fused_computation.101 | output fusion | flops 7340032 | bytes 8388608 | tf_op jit(solution)/shard_map/jit(cumsum)/reduce_window_sum | solution.py:57
  151.1 0.5 copy-done.1
  151.6 1.9 %slice.271 = f32[1,16,64,128]{3,2,1,0:T(8,128)} slice(f32[8,16,64,128]{3,2,1,0:T(8,128)} %fusion.31), slice={[7:8], [0:16], [0:64], [0:128]} | slice | bytes 1048576 | tf_op jit(solution)/shard_map/slice | solution.py:58
  153.5 0.0 all-gather.3.cloned.1.call-update
  153.5 17.3 %all-gather.3.cloned.1.call-done = f32[2,16,64,128]{3,2,1,0:T(8,128)} async-done(((f32[1,16,64,128]{3,2,1,0:T(8,128)}), f32[2,16,64,128]{3,2,1,0:T(8,128)}) %all-gather.3.cloned.1.call-update) | async-done | bytes 1048592 | tf_op jit(solution)/shard_map/all_gather | solution.py:24
  170.9 5.1 %add_multiply_fusion = f32[8,16,64,128]{3,2,1,0:T(8,128)} fusion(f32[8,16,64,128]{3,2,1,0:T(8,128)} %fusion.31, f32[16,64,128]{2,1,0:T(8,128)S(1)} %bitcast.9), kind=kLoop, calls=%fused_computation.74 | loop fusion | flops 2097152 | bytes 8912896 | tf_op jit(solution)/shard_map/div | solution.py:64
  (15 shorter events, 0.2 us)
Async XLA Ops:
  7.2 163.7 %all-gather.3.cloned.1.call-start = ((), (), s32[]{:S(2)}) async-start(), calls=%async_computation | async-start | bytes 1572864 | tf_op jit(solution)/shard_map/all_gather | solution.py:24
  8.5 16.0 %collective-permute-start = (f32[1,16,64,128]{3,2,1,0:T(8,128)S(1)}, f32[1,16,64,128]{3,2,1,0:T(8,128)S(1)}, u32[]{:S(2)}, u32[]{:S(2)}) collective-permute-start(f32[1,16,64,128]{3,2,1,0:T(8,128)S(1)} %get-tuple-element.65), channel_id=1, source_target_pairs={{0,16},{1,17},{2,18},{3,19},{4,20},{5,21},{6,22},{7,23},{8,24},{9,... | collective-permute-start | bytes 1572872 | tf_op jit(solution)/shard_map/ppermute | solution.py:16
  13.4 15.3 %collective-permute-start.1 = (f32[1,16,64,128]{3,2,1,0:T(8,128)S(1)}, f32[1,16,64,128]{3,2,1,0:T(8,128)S(1)}, u32[]{:S(2)}, u32[]{:S(2)}) collective-permute-start(f32[1,16,64,128]{3,2,1,0:T(8,128)S(1)} %get-tuple-element.64), channel_id=1, source_target_pairs={{16,0},{17,1},{18,2},{19,3},{20,4},{21,5},{22,6},{23,7},{24,8},{25... | collective-permute-start | bytes 1572872 | tf_op jit(solution)/shard_map/ppermute | solution.py:17
  28.7 24.2 %copy-start.2 = (f32[1,16,64,128]{3,2,1,0:T(8,128)}, f32[1,16,64,128]{3,2,1,0:T(8,128)S(1)}, u32[]{:S(2)}) copy-start(f32[1,16,64,128]{3,2,1,0:T(8,128)S(1)} %collective-permute-done.1) | copy-start | bytes 1572868
  28.7 24.9 %copy-start = (f32[8,16,64,128]{3,2,1,0:T(8,128)S(1)}, f32[8,16,64,128]{3,2,1,0:T(8,128)}, u32[]{:S(2)}) copy-start(f32[8,16,64,128]{3,2,1,0:T(8,128)} %param.5) | copy-start | bytes 12582916
  28.8 9.6 %collective-permute-start.2 = (f32[10,1,64,128]{3,2,1,0:T(8,128)S(1)}, f32[10,1,64,128]{3,2,1,0:T(8,128)S(1)}, u32[]{:S(2)}, u32[]{:S(2)}) collective-permute-start(f32[10,1,64,128]{3,2,1,0:T(8,128)S(1)} %get-tuple-element.58), channel_id=1, source_target_pairs={{0,4},{4,8},{8,12},{1,5},{5,9},{9,13},{2,6},{6,10},{10,14},{3,7},{... | collective-permute-start | bytes 983048 | tf_op jit(solution)/shard_map/ppermute | solution.py:16
  32.6 9.9 %collective-permute-start.3 = (f32[10,1,64,128]{3,2,1,0:T(8,128)S(1)}, f32[10,1,64,128]{3,2,1,0:T(8,128)S(1)}, u32[]{:S(2)}, u32[]{:S(2)}) collective-permute-start(f32[10,1,64,128]{3,2,1,0:T(8,128)S(1)} %get-tuple-element.59), channel_id=1, source_target_pairs={{4,0},{8,4},{12,8},{5,1},{9,5},{13,9},{6,2},{10,6},{14,10},{7,3},{... | collective-permute-start | bytes 983048 | tf_op jit(solution)/shard_map/ppermute | solution.py:17
  42.5 10.4 %copy-start.3 = (f32[10,1,64,128]{3,2,1,0:T(8,128)}, f32[10,1,64,128]{3,2,1,0:T(8,128)S(1)}, u32[]{:S(2)}) copy-start(f32[10,1,64,128]{3,2,1,0:T(8,128)S(1)} %collective-permute-done.3) | copy-start | bytes 983044
  42.7 5.9 %collective-permute-start.4 = (f32[10,18,1,128]{3,1,2,0:T(8,128)S(1)}, f32[10,18,1,128]{3,1,2,0:T(8,128)S(1)}, u32[]{:S(2)}, u32[]{:S(2)}) collective-permute-start(f32[10,18,1,128]{3,1,2,0:T(8,128)S(1)} %copy.22), channel_id=1, source_target_pairs={{0,2},{1,3},{4,6},{5,7},{8,10},{9,11},{12,14},{13,15},{16,18},{17,... | collective-permute-start | bytes 276488 | tf_op jit(solution)/shard_map/ppermute | solution.py:16
  46.1 6.8 %collective-permute-start.5 = (f32[10,18,1,128]{3,1,2,0:T(8,128)S(1)}, f32[10,18,1,128]{3,1,2,0:T(8,128)S(1)}, u32[]{:S(2)}, u32[]{:S(2)}) collective-permute-start(f32[10,18,1,128]{3,1,2,0:T(8,128)S(1)} %copy.24), channel_id=1, source_target_pairs={{2,0},{3,1},{6,4},{7,5},{10,8},{11,9},{14,12},{15,13},{18,16},{19,... | collective-permute-start | bytes 276488 | tf_op jit(solution)/shard_map/ppermute | solution.py:17
  62.1 10.8 %collective-permute-start.6 = (f32[1,16,64,128]{3,2,1,0:T(8,128)S(1)}, f32[1,16,64,128]{3,2,1,0:T(8,128)S(1)}, u32[]{:S(2)}, u32[]{:S(2)}) collective-permute-start(f32[1,16,64,128]{3,2,1,0:T(8,128)S(1)} %get-tuple-element.62), channel_id=1, source_target_pairs={{0,16},{1,17},{2,18},{3,19},{4,20},{5,21},{6,22},{7,23},{8,24},{9,... | collective-permute-start | bytes 1572872 | tf_op jit(solution)/shard_map/ppermute | solution.py:16
  65.2 11.9 %collective-permute-start.7 = (f32[1,16,64,128]{3,2,1,0:T(8,128)S(1)}, f32[1,16,64,128]{3,2,1,0:T(8,128)S(1)}, u32[]{:S(2)}, u32[]{:S(2)}) collective-permute-start(f32[1,16,64,128]{3,2,1,0:T(8,128)S(1)} %get-tuple-element.63), channel_id=1, source_target_pairs={{16,0},{17,1},{18,2},{19,3},{20,4},{21,5},{22,6},{23,7},{24,8},{25... | collective-permute-start | bytes 1572872 | tf_op jit(solution)/shard_map/ppermute | solution.py:17
  77.1 8.0 %collective-permute-start.8 = (f32[10,1,64,128]{3,2,1,0:T(8,128)S(1)}, f32[10,1,64,128]{3,2,1,0:T(8,128)S(1)}, u32[]{:S(2)}, u32[]{:S(2)}) collective-permute-start(f32[10,1,64,128]{3,2,1,0:T(8,128)S(1)} %get-tuple-element.56), channel_id=1, source_target_pairs={{0,4},{4,8},{8,12},{1,5},{5,9},{9,13},{2,6},{6,10},{10,14},{3,7},{... | collective-permute-start | bytes 983048 | tf_op jit(solution)/shard_map/ppermute | solution.py:16
  80.6 9.0 %collective-permute-start.9 = (f32[10,1,64,128]{3,2,1,0:T(8,128)S(1)}, f32[10,1,64,128]{3,2,1,0:T(8,128)S(1)}, u32[]{:S(2)}, u32[]{:S(2)}) collective-permute-start(f32[10,1,64,128]{3,2,1,0:T(8,128)S(1)} %get-tuple-element.57), channel_id=1, source_target_pairs={{4,0},{8,4},{12,8},{5,1},{9,5},{13,9},{6,2},{10,6},{14,10},{7,3},{... | collective-permute-start | bytes 983048 | tf_op jit(solution)/shard_map/ppermute | solution.py:17
  89.7 4.2 %collective-permute-start.10 = (f32[10,18,1,128]{3,1,2,0:T(8,128)S(1)}, f32[10,18,1,128]{3,1,2,0:T(8,128)S(1)}, u32[]{:S(2)}, u32[]{:S(2)}) collective-permute-start(f32[10,18,1,128]{3,1,2,0:T(8,128)S(1)} %copy.26), channel_id=1, source_target_pairs={{0,2},{1,3},{4,6},{5,7},{8,10},{9,11},{12,14},{13,15},{16,18},{17,... | collective-permute-start | bytes 276488 | tf_op jit(solution)/shard_map/ppermute | solution.py:16
  91.5 6.8 %collective-permute-start.11 = (f32[10,18,1,128]{3,1,2,0:T(8,128)S(1)}, f32[10,18,1,128]{3,1,2,0:T(8,128)S(1)}, u32[]{:S(2)}, u32[]{:S(2)}) collective-permute-start(f32[10,18,1,128]{3,1,2,0:T(8,128)S(1)} %copy.28), channel_id=1, source_target_pairs={{2,0},{3,1},{6,4},{7,5},{10,8},{11,9},{14,12},{15,13},{18,16},{19,... | collective-permute-start | bytes 276488 | tf_op jit(solution)/shard_map/ppermute | solution.py:17
  106.4 8.1 %collective-permute-start.12 = (f32[1,16,64,128]{3,2,1,0:T(8,128)S(1)}, f32[1,16,64,128]{3,2,1,0:T(8,128)S(1)}, u32[]{:S(2)}, u32[]{:S(2)}) collective-permute-start(f32[1,16,64,128]{3,2,1,0:T(8,128)S(1)} %get-tuple-element.60), channel_id=1, source_target_pairs={{0,16},{1,17},{2,18},{3,19},{4,20},{5,21},{6,22},{7,23},{8,24},{9,... | collective-permute-start | bytes 1572872 | tf_op jit(solution)/shard_map/ppermute | solution.py:16
  107.9 11.1 %collective-permute-start.13 = (f32[1,16,64,128]{3,2,1,0:T(8,128)S(1)}, f32[1,16,64,128]{3,2,1,0:T(8,128)S(1)}, u32[]{:S(2)}, u32[]{:S(2)}) collective-permute-start(f32[1,16,64,128]{3,2,1,0:T(8,128)S(1)} %get-tuple-element.61), channel_id=1, source_target_pairs={{16,0},{17,1},{18,2},{19,3},{20,4},{21,5},{22,6},{23,7},{24,8},{25... | collective-permute-start | bytes 1572872 | tf_op jit(solution)/shard_map/ppermute | solution.py:17
  119.1 8.0 %collective-permute-start.14 = (f32[10,1,64,128]{3,2,1,0:T(8,128)S(1)}, f32[10,1,64,128]{3,2,1,0:T(8,128)S(1)}, u32[]{:S(2)}, u32[]{:S(2)}) collective-permute-start(f32[10,1,64,128]{3,2,1,0:T(8,128)S(1)} %get-tuple-element.54), channel_id=1, source_target_pairs={{0,4},{4,8},{8,12},{1,5},{5,9},{9,13},{2,6},{6,10},{10,14},{3,7},{... | collective-permute-start | bytes 983048 | tf_op jit(solution)/shard_map/ppermute | solution.py:16
  122.6 9.0 %collective-permute-start.15 = (f32[10,1,64,128]{3,2,1,0:T(8,128)S(1)}, f32[10,1,64,128]{3,2,1,0:T(8,128)S(1)}, u32[]{:S(2)}, u32[]{:S(2)}) collective-permute-start(f32[10,1,64,128]{3,2,1,0:T(8,128)S(1)} %get-tuple-element.55), channel_id=1, source_target_pairs={{4,0},{8,4},{12,8},{5,1},{9,5},{13,9},{6,2},{10,6},{14,10},{7,3},{... | collective-permute-start | bytes 983048 | tf_op jit(solution)/shard_map/ppermute | solution.py:17
  131.7 3.9 %collective-permute-start.16 = (f32[10,18,1,128]{3,1,2,0:T(8,128)S(1)}, f32[10,18,1,128]{3,1,2,0:T(8,128)S(1)}, u32[]{:S(2)}, u32[]{:S(2)}) collective-permute-start(f32[10,18,1,128]{3,1,2,0:T(8,128)S(1)} %copy.30), channel_id=1, source_target_pairs={{0,2},{1,3},{4,6},{5,7},{8,10},{9,11},{12,14},{13,15},{16,18},{17,... | collective-permute-start | bytes 276488 | tf_op jit(solution)/shard_map/ppermute | solution.py:16
  133.2 6.8 %collective-permute-start.17 = (f32[10,18,1,128]{3,1,2,0:T(8,128)S(1)}, f32[10,18,1,128]{3,1,2,0:T(8,128)S(1)}, u32[]{:S(2)}, u32[]{:S(2)}) collective-permute-start(f32[10,18,1,128]{3,1,2,0:T(8,128)S(1)} %copy.32), channel_id=1, source_target_pairs={{2,0},{3,1},{6,4},{7,5},{10,8},{11,9},{14,12},{15,13},{18,16},{19,... | collective-permute-start | bytes 276488 | tf_op jit(solution)/shard_map/ppermute | solution.py:17
  148.3 3.3 %copy-start.1 = (f32[8,16,64,128]{3,2,1,0:T(8,128)}, f32[8,16,64,128]{3,2,1,0:T(8,128)S(1)}, u32[]{:S(2)}) copy-start(f32[8,16,64,128]{3,2,1,0:T(8,128)S(1)} %fusion.4) | copy-start | bytes 12582916
Sparse Core Ops, SparseCore 0:
  153.6 17.1 all-gather.2
where the time goes:
time: 184 us; the launch traced here: 183 us
  waiting for transfers between devices  89.2 us (48%)
  starting transfers between devices  38.6 us (21%)
  other arithmetic  32.8 us (18%)
  between operations  14.4 us (8%)
  local copies, waits for them, and re-layouts  7.85 us (4%)
    ppermute x9, waiting for transfers between devices, padded_2(): after = lax.ppermute(initial, axis, down)  35.9 us
    ppermute x9, waiting for transfers between devices, padded_2(): before = lax.ppermute(last, axis, up)  35.9 us
    ppermute x9, starting transfers between devices, padded_2(): before = lax.ppermute(last, axis, up)  27 us
    add x3, other arithmetic, march_step(): return middle + 0.1 * spread + 0.2 * middle * (1.0 - middle * crowding)  24.5 us
    all_gather x1, waiting for transfers between devices, entering(): gathered = lax.all_gather(part, axis)  17.3 us
    ppermute x9, starting transfers between devices, padded_2(): after = lax.ppermute(initial, axis, down)  11.6 us
    div x1, other arithmetic, on_device(): potential = (here + below) / (field_values.shape[0] * lax.axis_size('rows'))  5.13 us
  transfers between devices with their start and end apart: 19, of which 19 were waited for; matrix products, arithmetic and copies ran while one was open for 2% of the time, Pallas kernels for 0%

commit v1 on v0

v1 whole, which is shorter than its diff:
```python
import functools

import jax
import jax.numpy as jnp
from jax import lax
from jax.experimental import pallas as pl
from jax.experimental.pallas import tpu as pltpu
from jax.sharding import PartitionSpec as P

STEPS = 3
MESH = pl.DeviceIdType.MESH
AXES = ("rows", "cols", "slabs")


def pieces_of(length):
    for count in (4, 2):
        if length % count == 0:
            return count
    return 1


def march_kernel(
    sizes, field, crowd, out_field, out_below,
    grid0, grid1, grid2, grid3, cells, y_in, y_out, total, below,
    x_send, x_recv, z_send, z_recv, y_send, y_recv, t_send, t_recv, load, store,
):
    J, I, K, L = field.shape
    grids = (grid0, grid1, grid2, grid3)
    Q = pieces_of(I)
    W = I // Q
    place = {axis: lax.axis_index(axis) for axis in AXES}
    has_target = {}
    has_source = {}
    for axis in AXES:
        later, earlier = place[axis] < sizes[axis] - 1, place[axis] > 0
        has_target[axis] = (later, earlier)
        has_source[axis] = (earlier, later)

    def target(axis, way):
        n = sizes[axis]
        return {axis: lax.rem(place[axis] + (1 if way == 0 else n - 1), n)}

    load_field = pltpu.make_async_copy(
        field, grid0.at[1 : J + 1, 1 : I + 1], load.at[0]
    )
    load_cells = pltpu.make_async_copy(crowd, cells, load.at[1])
    load_field.start()

    barrier = pltpu.get_barrier_semaphore()
    for axis in AXES:
        if sizes[axis] > 1:
            for way in (0, 1):

                @pl.when(has_target[axis][way])
                def _():
                    pl.semaphore_signal(
                        barrier, inc=1, device_id=target(axis, way), device_id_type=MESH
                    )

    peers = jnp.int32(0)
    for axis in AXES:
        if sizes[axis] > 1:
            for way in (0, 1):
                peers = peers + has_source[axis][way].astype(jnp.int32)
    pl.semaphore_wait(barrier, peers)

    def x_copy(step, way, q):
        plane = J - 1 if way == 0 else 0
        halo = 0 if way == 0 else J + 1
        columns = pl.ds(1 + q * W, W)
        if step == 0:
            source = field.at[plane, pl.ds(q * W, W)]
        else:
            source = grids[step].at[1 + plane, columns]
        return pltpu.make_async_remote_copy(
            src_ref=source,
            dst_ref=grids[step].at[halo, columns],
            send_sem=x_send.at[step, way, q],
            recv_sem=x_recv.at[step, way, q],
            device_id=target("rows", way),
            device_id_type=MESH,
        )

    parts = ((0, 1), (1, J - 2), (J - 1, 1))

    def z_copy(step, way, part):
        first, count = parts[part]
        column = I - 1 if way == 0 else 0
        halo = 0 if way == 0 else I + 1
        if step == 0:
            source = field.at[pl.ds(first, count), column]
        else:
            source = grids[step].at[pl.ds(1 + first, count), 1 + column]
        return pltpu.make_async_remote_copy(
            src_ref=source,
            dst_ref=grids[step].at[pl.ds(1 + first, count), halo],
            send_sem=z_send.at[step, way, part],
            recv_sem=z_recv.at[step, way, part],
            device_id=target("cols", way),
            device_id_type=MESH,
        )

    def y_copy(step, way):
        return pltpu.make_async_remote_copy(
            src_ref=y_out.at[step, 1 - way],
            dst_ref=y_in.at[step, way],
            send_sem=y_send.at[step, way],
            recv_sem=y_recv.at[step, way],
            device_id=target("slabs", way),
            device_id_type=MESH,
        )

    def t_copy(q):
        columns = pl.ds(q * W, W)
        return pltpu.make_async_remote_copy(
            src_ref=total.at[columns],
            dst_ref=below.at[columns],
            send_sem=t_send.at[q],
            recv_sem=t_recv.at[q],
            device_id=target("rows", 0),
            device_id_type=MESH,
        )

    def start(axis, way, copies):
        if sizes[axis] > 1:

            @pl.when(has_target[axis][way])
            def _():
                for one in copies:
                    one.start()

    def sent(axis, way, copies):
        if sizes[axis] > 1:

            @pl.when(has_target[axis][way])
            def _():
                for one in copies:
                    one.wait_send()

    def arrived(axis, way, copies):
        if sizes[axis] > 1:

            @pl.when(has_source[axis][way])
            def _():
                for one in copies:
                    one.wait_recv()

    for way in (0, 1):
        start("cols", way, [z_copy(0, way, part) for part in range(3)])
    for q in range(Q):
        for way in (0, 1):
            start("rows", way, [x_copy(0, way, q)])
    load_cells.start()

    zero = jnp.zeros((K, L), jnp.float32)
    for way in (0, 1):

        @pl.when(jnp.logical_not(has_source["rows"][way]))
        def _():
            def body(i, _):
                for step in range(STEPS):
                    grids[step][0 if way == 0 else J + 1, 1 + i] = zero
                if way == 0:
                    below[i] = zero
                return 0

            lax.fori_loop(0, I, body, 0)

        @pl.when(jnp.logical_not(has_source["cols"][way]))
        def _():
            def body(j, _):
                for step in range(STEPS):
                    grids[step][1 + j, 0 if way == 0 else I + 1] = zero
                return 0

            lax.fori_loop(0, J, body, 0)

        @pl.when(jnp.logical_not(has_source["slabs"][way]))
        def _():
            for step in range(STEPS):
                y_in[step, way] = jnp.zeros((J, I, L), jnp.float32)

    load_field.wait()

    def rims(step, j, i, value):
        y_out[step, 0, j, pl.ds(i, 1), :] = value[0:1]
        y_out[step, 1, j, pl.ds(i, 1), :] = value[K - 1 : K]

    def first_rims(j, _):
        def body(i, _):
            for side, row in ((0, 0), (1, K - 1)):
                y_out[0, side, j, pl.ds(i, 1), :] = grid0[1 + j, 1 + i, pl.ds(row, 1), :]
            return 0

        return lax.fori_loop(0, I, body, 0)

    lax.fori_loop(0, J, first_rims, 0)
    for way in (0, 1):
        start("slabs", way, [y_copy(0, way)])
    load_cells.wait()

    def tile(step, j, i):
        old, new = grids[step - 1], grids[step]
        middle = old[1 + j, 1 + i]
        before = y_in[step - 1, 0, j, pl.ds(i, 1), :]
        after = y_in[step - 1, 1, j, pl.ds(i, 1), :]
        near = jnp.concatenate([before, middle[: K - 1]], axis=0)
        far = jnp.concatenate([middle[1:], after], axis=0)
        around = (
            (old[j, 1 + i] + old[2 + j, 1 + i])
            + (old[1 + j, i] + old[1 + j, 2 + i])
            + (near + far)
        )
        value = middle * (0.6 - 0.2 * (middle * cells[j, i])) + 0.1 * around
        if step < STEPS:
            new[1 + j, 1 + i] = value
            rims(step, j, i, value)
        else:
            new[j, i] = value

    for step in range(1, STEPS + 1):
        last = step == STEPS
        for way in (0, 1):
            arrived("slabs", way, [y_copy(step - 1, way)])

        def inner(j, _):
            def body(i, _):
                tile(step, j, i)
                return 0

            return lax.fori_loop(1, I - 1, body, 0)

        lax.fori_loop(1, J - 1, inner, 0)
        for way in (0, 1):
            arrived("cols", way, [z_copy(step - 1, way, part) for part in range(3)])

        def edges(j, _):
            tile(step, j, 0)
            tile(step, j, I - 1)
            return 0

        lax.fori_loop(1, J - 1, edges, 0)
        if not last:
            for way in (0, 1):
                start("cols", way, [z_copy(step, way, 1)])
        for q in range(Q):
            for way in (0, 1):
                arrived("rows", way, [x_copy(step - 1, way, q)])

            def faces(i, _):
                tile(step, 0, i)
                tile(step, J - 1, i)
                return 0

            lax.fori_loop(q * W, (q + 1) * W, faces, 0)
            if not last:
                for way in (0, 1):
                    start("rows", way, [x_copy(step, way, q)])
            else:
                columns = pl.ds(q * W, W)

                @pl.when(has_target["rows"][0])
                def _():
                    def add(i, _):
                        value = grid3[0, i]
                        for j in range(1, J):
                            value = value + grid3[j, i]
                        total[i] = value
                        return 0

                    lax.fori_loop(q * W, (q + 1) * W, add, 0)

                @pl.when(jnp.logical_not(has_source["rows"][0]))
                def _():
                    start("rows", 0, [t_copy(q)])

                pltpu.make_async_copy(
                    grid3.at[:, columns], out_field.at[:, columns], store.at[0, q]
                ).start()
        if not last:
            for way in (0, 1):
                start("cols", way, [z_copy(step, way, 0), z_copy(step, way, 2)])
                start("slabs", way, [y_copy(step, way)])

    for q in range(Q):
        columns = pl.ds(q * W, W)

        @pl.when(has_source["rows"][0])
        def _():
            if sizes["rows"] > 1:
                t_copy(q).wait_recv()

                @pl.when(has_target["rows"][0])
                def _():
                    def add(i, _):
                        total[i] = total[i] + below[i]
                        return 0

                    lax.fori_loop(q * W, (q + 1) * W, add, 0)
                    t_copy(q).start()

        pltpu.make_async_copy(
            below.at[columns], out_below.at[columns], store.at[1, q]
        ).start()

    for step in range(STEPS):
        for way in (0, 1):
            sent("rows", way, [x_copy(step, way, q) for q in range(Q)])
            sent("cols", way, [z_copy(step, way, part) for part in range(3)])
            sent("slabs", way, [y_copy(step, way)])
    sent("rows", 0, [t_copy(q) for q in range(Q)])
    for q in range(Q):
        columns = pl.ds(q * W, W)
        pltpu.make_async_copy(
            grid3.at[:, columns], out_field.at[:, columns], store.at[0, q]
        ).wait()
        pltpu.make_async_copy(
            below.at[columns], out_below.at[columns], store.at[1, q]
        ).wait()


def sum_kernel(scale, field, below, potential, field_end):
    J, W = field.shape[0], field.shape[1]

    def body(i, _):
        value = below[i]
        for j in range(J):
            here = field[j, i]
            field_end[j, i] = here
            value = value + here
            potential[j, i] = value * scale
        return 0

    lax.fori_loop(0, W, body, 0)


def solution(mesh):
    sizes = {axis: mesh.shape[axis] for axis in AXES}

    def on_device(field_values, crowding):
        J, I, K, L = field_values.shape
        Q = pieces_of(I)
        padded = pltpu.VMEM((J + 2, I + 2, K, L), jnp.float32)
        block = jax.ShapeDtypeStruct((J, I, K, L), jnp.float32)
        plane = jax.ShapeDtypeStruct((I, K, L), jnp.float32)
        anywhere = pl.BlockSpec(memory_space=pl.ANY)
        dma = pltpu.SemaphoreType.DMA
        field_end, below = pl.pallas_call(
            functools.partial(march_kernel, sizes),
            out_shape=(block, plane),
            in_specs=[anywhere] * 2,
            out_specs=(anywhere, anywhere),
            scratch_shapes=[
                padded,
                padded,
                padded,
                pltpu.VMEM((J, I, K, L), jnp.float32),
                pltpu.VMEM((J, I, K, L), jnp.float32),
                pltpu.VMEM((STEPS, 2, J, I, L), jnp.float32),
                pltpu.VMEM((STEPS, 2, J, I, L), jnp.float32),
                pltpu.VMEM((I, K, L), jnp.float32),
                pltpu.VMEM((I, K, L), jnp.float32),
                dma((STEPS, 2, Q)),
                dma((STEPS, 2, Q)),
                dma((STEPS, 2, 3)),
                dma((STEPS, 2, 3)),
                dma((STEPS, 2)),
                dma((STEPS, 2)),
                dma((Q,)),
                dma((Q,)),
                dma((2,)),
                dma((2, Q)),
            ],
            compiler_params=pltpu.CompilerParams(
                collective_id=0,
                has_side_effects=True,
                vmem_limit_bytes=60 * 1024 * 1024,
            ),
        )(field_values, crowding)

        W = 2 if I % 2 == 0 else 1
        spec = pl.BlockSpec((J, W, K, L), lambda i: (0, i, 0, 0))
        potential, field_end = pl.pallas_call(
            functools.partial(sum_kernel, 1.0 / (J * sizes["rows"])),
            out_shape=(block, block),
            grid=(I // W,),
            in_specs=[spec, pl.BlockSpec((W, K, L), lambda i: (i, 0, 0))],
            out_specs=(spec, spec),
        )(field_end, below)
        return potential, field_end

    spec = P(("trial", "rows"), "cols", "slabs", None)
    return jax.shard_map(
        on_device,
        mesh=mesh,
        in_specs=(spec, spec),
        out_specs=(spec, spec),
        check_vma=False,
    )
```

time: 184 us -> 57.7 us (0.31)
  waiting for transfers between devices: 89.2 us -> 0 us
  Pallas kernels: 0 us -> 56.6 us
  starting transfers between devices: 38.6 us -> 0 us
  other arithmetic: 32.8 us -> 0 us
  between operations: 14.4 us -> 0.64 us
  local copies, waits for them, and re-layouts: 7.85 us -> 0 us
    ppermute x18 -> x0, waiting for transfers between devices: 71.8 us -> none  [the longest x9 35.9 us: padded_2(): after = lax.ppermute(initial, axis, down)]
    pallas_call x0 -> x2, Pallas kernels: none -> 56.6 us  [the longest x1 49.3 us: on_device(): pl.pallas_call(functools.partial(march_kernel, sizes), out_shape=(block,...]
    ppermute x18 -> x0, starting transfers between devices: 38.6 us -> none  [the longest x9 27 us: padded_2(): before = lax.ppermute(last, axis, up)]
    add x3 -> x0, other arithmetic: 24.5 us -> none  [march_step(): return middle + 0.1 * spread + 0.2 * middle * (1.0 - middle * crowding)]
    all_gather x1 -> x0, waiting for transfers between devices: 17.3 us -> none  [entering(): gathered = lax.all_gather(part, axis)]
    div x1 -> x0, other arithmetic: 5.13 us -> none  [on_device(): potential = (here + below) / (field_values.shape[0] * lax.axis_size('rows'))]
    slice x11 -> x0, local copies, waits for them, and re-layouts: 3.48 us -> none  [the longest x1 1.9 us: on_device(): total = lax.slice_in_dim(here, here.shape[0] - 1, here.shape[0], axis=0)]
    unnamed x10 -> x0, local copies, waits for them, and re-layouts: 3.08 us -> none
  transfers between devices with their start and end apart: 19 -> 0, of which waited for: 19 -> 0; matrix products, arithmetic and copies ran while one was open for 2% -> 0% of each run, Pallas kernels for 0% -> 0%
where the time goes in v1:
time: 57.7 us; the launch traced here: 57.2 us
  Pallas kernels  56.6 us (98%)
  between operations  0.64 us (1%)
    pallas_call x1, Pallas kernels, on_device(): pl.pallas_call(functools.partial(march_kernel, sizes), out_shape=(block,...  49.3 us
    pallas_call x1, Pallas kernels, on_device(): pl.pallas_call(functools.partial(sum_kernel, 1.0 / (J * sizes['rows'])),...  7.35 us

profile of v1, /device:TPU:0, one launch (start us, length us, event | category | flops | bytes accessed | tf_op | source)
XLA Modules:
  0.0 57.2 jit_solution(17651173350382124567)
XLA Ops:
  0.6 49.3 %shard_map.41 = (f32[8,16,64,128]{3,2,1,0:T(8,128)}, f32[16,64,128]{2,1,0:T(8,128)}) custom-call(f32[8,16,64,128]{3,2,1,0:T(8,128)} %field.1, f32[8,16,64,128]{3,2,1,0:T(8,128)} %crowd.1), custom_call_target="tpu_custom_call" | custom-call | tf_op jit(solution)/shard_map/pallas_call | solution.py:348
  49.9 7.3 %shard_map.42 = (f32[8,16,64,128]{3,2,1,0:T(8,128)}, f32[8,16,64,128]{3,2,1,0:T(8,128)}) custom-call(f32[8,16,64,128]{3,2,1,0:T(8,128)} %get-tuple-element.4.field, f32[16,64,128]{2,1,0:T(8,128)} %get-tuple-element.5.below), custom_call_target="tpu_custom_call" | custom-call | tf_op jit(solution)/shard_map/pallas_call | solution.py:383

commit v2 on v1

--- a/solution.py
+++ b/solution.py
@@ -20,9 +20,9 @@
 
 
 def march_kernel(
-    sizes, field, crowd, out_field, out_below,
-    grid0, grid1, grid2, grid3, cells, y_in, y_out, total, below,
-    x_send, x_recv, z_send, z_recv, y_send, y_recv, t_send, t_recv, load, store,
+    sizes, field, crowd, grid3, out_below,
+    grid0, grid1, grid2, cells, y_in, y_out, total, below,
+    x_send, x_recv, z_send, z_recv, y_send, y_recv, t_send, t_recv, load,
 ):
     J, I, K, L = field.shape
     grids = (grid0, grid1, grid2, grid3)
@@ -257,7 +257,6 @@
                 for way in (0, 1):
                     start("rows", way, [x_copy(step, way, q)])
             else:
-                columns = pl.ds(q * W, W)
 
                 @pl.when(has_target["rows"][0])
                 def _():
@@ -273,17 +272,12 @@
                 @pl.when(jnp.logical_not(has_source["rows"][0]))
                 def _():
                     start("rows", 0, [t_copy(q)])
-
-                pltpu.make_async_copy(
-                    grid3.at[:, columns], out_field.at[:, columns], store.at[0, q]
-                ).start()
         if not last:
             for way in (0, 1):
                 start("cols", way, [z_copy(step, way, 0), z_copy(step, way, 2)])
                 start("slabs", way, [y_copy(step, way)])
 
     for q in range(Q):
-        columns = pl.ds(q * W, W)
 
         @pl.when(has_source["rows"][0])
         def _():
@@ -299,9 +293,8 @@
                     lax.fori_loop(q * W, (q + 1) * W, add, 0)
                     t_copy(q).start()
 
-        pltpu.make_async_copy(
-            below.at[columns], out_below.at[columns], store.at[1, q]
-        ).start()
+        columns = pl.ds(q * W, W)
+        out_below[columns] = below[columns]
 
     for step in range(STEPS):
         for way in (0, 1):
@@ -309,29 +302,34 @@
             sent("cols", way, [z_copy(step, way, part) for part in range(3)])
             sent("slabs", way, [y_copy(step, way)])
     sent("rows", 0, [t_copy(q) for q in range(Q)])
+
+def sum_kernel(scale, field, below, potential, field_end, sums, end_sem, sum_sem):
+    J, I = field.shape[0], field.shape[1]
+    Q = pieces_of(I)
+    W = I // Q
+    whole = pltpu.make_async_copy(field, field_end, end_sem)
+    whole.start()
+
+    def piece(q):
+        columns = pl.ds(q * W, W)
+        return pltpu.make_async_copy(
+            sums.at[:, columns], potential.at[:, columns], sum_sem.at[q]
+        )
+
     for q in range(Q):
-        columns = pl.ds(q * W, W)
-        pltpu.make_async_copy(
-            grid3.at[:, columns], out_field.at[:, columns], store.at[0, q]
-        ).wait()
-        pltpu.make_async_copy(
-            below.at[columns], out_below.at[columns], store.at[1, q]
-        ).wait()
-
-
-def sum_kernel(scale, field, below, potential, field_end):
-    J, W = field.shape[0], field.shape[1]
-
-    def body(i, _):
-        value = below[i]
-        for j in range(J):
-            here = field[j, i]
-            field_end[j, i] = here
-            value = value + here
-            potential[j, i] = value * scale
-        return 0
-
-    lax.fori_loop(0, W, body, 0)
+
+        def body(i, _):
+            value = below[i]
+            for j in range(J):
+                value = value + field[j, i]
+                sums[j, i] = value * scale
+            return 0
+
+        lax.fori_loop(q * W, (q + 1) * W, body, 0)
+        piece(q).start()
+    for q in range(Q):
+        piece(q).wait()
+    whole.wait()
 
 
 def solution(mesh):
@@ -342,19 +340,21 @@
         Q = pieces_of(I)
         padded = pltpu.VMEM((J + 2, I + 2, K, L), jnp.float32)
         block = jax.ShapeDtypeStruct((J, I, K, L), jnp.float32)
-        plane = jax.ShapeDtypeStruct((I, K, L), jnp.float32)
+        vector = pl.BlockSpec(memory_space=pltpu.VMEM)
         anywhere = pl.BlockSpec(memory_space=pl.ANY)
         dma = pltpu.SemaphoreType.DMA
         field_end, below = pl.pallas_call(
             functools.partial(march_kernel, sizes),
-            out_shape=(block, plane),
+            out_shape=(
+                pltpu.VMEM((J, I, K, L), jnp.float32),
+                pltpu.VMEM((I, K, L), jnp.float32),
+            ),
             in_specs=[anywhere] * 2,
-            out_specs=(anywhere, anywhere),
+            out_specs=(vector, vector),
             scratch_shapes=[
                 padded,
                 padded,
                 padded,
-                pltpu.VMEM((J, I, K, L), jnp.float32),
                 pltpu.VMEM((J, I, K, L), jnp.float32),
                 pltpu.VMEM((STEPS, 2, J, I, L), jnp.float32),
                 pltpu.VMEM((STEPS, 2, J, I, L), jnp.float32),
@@ -369,23 +369,21 @@
                 dma((Q,)),
                 dma((Q,)),
                 dma((2,)),
-                dma((2, Q)),
             ],
             compiler_params=pltpu.CompilerParams(
                 collective_id=0,
                 has_side_effects=True,
-                vmem_limit_bytes=60 * 1024 * 1024,
+                vmem_limit_bytes=57 * 1024 * 1024,
             ),
         )(field_values, crowding)
 
-        W = 2 if I % 2 == 0 else 1
-        spec = pl.BlockSpec((J, W, K, L), lambda i: (0, i, 0, 0))
         potential, field_end = pl.pallas_call(
             functools.partial(sum_kernel, 1.0 / (J * sizes["rows"])),
             out_shape=(block, block),
-            grid=(I // W,),
-            in_specs=[spec, pl.BlockSpec((W, K, L), lambda i: (i, 0, 0))],
-            out_specs=(spec, spec),
+            in_specs=[vector, vector],
+            out_specs=(anywhere, anywhere),
+            scratch_shapes=[pltpu.VMEM((J, I, K, L), jnp.float32), dma, dma((Q,))],
+            compiler_params=pltpu.CompilerParams(vmem_limit_bytes=16 * 1024 * 1024),
         )(field_end, below)
         return potential, field_end
 

time: 57.7 us -> 53.3 us (0.924)
  Pallas kernels: 56.6 us -> 52.5 us
    pallas_call x1, Pallas kernels: 7.35 us -> 3.34 us  [on_device(): pl.pallas_call(functools.partial(sum_kernel, 1.0 / (J * sizes['rows'])),...]
where the time goes in v2:
time: 53.3 us; the launch traced here: 53.2 us
  Pallas kernels  52.5 us (98%)
  between operations  0.64 us (1%)
    pallas_call x1, Pallas kernels, on_device(): pl.pallas_call(functools.partial(march_kernel, sizes), out_shape=(pltpu.V...  49.2 us
    pallas_call x1, Pallas kernels, on_device(): pl.pallas_call(functools.partial(sum_kernel, 1.0 / (J * sizes['rows'])),...  3.34 us

profile of v2, /device:TPU:0, one launch (start us, length us, event | category | flops | bytes accessed | tf_op | source)
XLA Modules:
  0.0 53.2 jit_solution(4940302212650314672)
XLA Ops:
  0.6 49.2 %shard_map.41 = (f32[8,16,64,128]{3,2,1,0:T(8,128)S(1)}, f32[16,64,128]{2,1,0:T(8,128)S(1)}) custom-call(f32[8,16,64,128]{3,2,1,0:T(8,128)} %field.1, f32[8,16,64,128]{3,2,1,0:T(8,128)} %crowd.1), custom_call_target="tpu_custom_call" | custom-call | tf_op jit(solution)/shard_map/pallas_call | solution.py:346
  49.8 3.3 %shard_map.42 = (f32[8,16,64,128]{3,2,1,0:T(8,128)}, f32[8,16,64,128]{3,2,1,0:T(8,128)}) custom-call(f32[8,16,64,128]{3,2,1,0:T(8,128)S(1)} %get-tuple-element.4.field, f32[16,64,128]{2,1,0:T(8,128)S(1)} %get-tuple-element.5.below), custom_call_target="tpu_custom_call" | custom-call | tf_op jit(solution)/shard_map/pallas_call | solution.py:380

commit v3 on v2

--- a/solution.py
+++ b/solution.py
@@ -12,8 +12,8 @@
 AXES = ("rows", "cols", "slabs")
 
 
-def pieces_of(length):
-    for count in (4, 2):
+def pieces_of(length, counts):
+    for count in counts:
         if length % count == 0:
             return count
     return 1
@@ -22,11 +22,11 @@
 def march_kernel(
     sizes, field, crowd, grid3, out_below,
     grid0, grid1, grid2, cells, y_in, y_out, total, below,
-    x_send, x_recv, z_send, z_recv, y_send, y_recv, t_send, t_recv, load,
+    x_send, x_recv, z_send, z_recv, y_send, y_recv, t_send, t_recv, load, face,
 ):
     J, I, K, L = field.shape
     grids = (grid0, grid1, grid2, grid3)
-    Q = pieces_of(I)
+    Q = pieces_of(I, (2,))
     W = I // Q
     place = {axis: lax.axis_index(axis) for axis in AXES}
     has_target = {}
@@ -40,11 +40,21 @@
         n = sizes[axis]
         return {axis: lax.rem(place[axis] + (1 if way == 0 else n - 1), n)}
 
+    def face_load(way, q):
+        plane = J - 1 if way == 0 else 0
+        return pltpu.make_async_copy(
+            field.at[plane, pl.ds(q * W, W)],
+            grid0.at[1 + plane, pl.ds(1 + q * W, W)],
+            face.at[way, q],
+        )
+
     load_field = pltpu.make_async_copy(
-        field, grid0.at[1 : J + 1, 1 : I + 1], load.at[0]
+        field.at[1 : J - 1], grid0.at[2:J, 1 : I + 1], load.at[0]
     )
     load_cells = pltpu.make_async_copy(crowd, cells, load.at[1])
-    load_field.start()
+    for q in range(Q):
+        for way in (0, 1):
+            face_load(way, q).start()
 
     barrier = pltpu.get_barrier_semaphore()
     for axis in AXES:
@@ -68,12 +78,8 @@
         plane = J - 1 if way == 0 else 0
         halo = 0 if way == 0 else J + 1
         columns = pl.ds(1 + q * W, W)
-        if step == 0:
-            source = field.at[plane, pl.ds(q * W, W)]
-        else:
-            source = grids[step].at[1 + plane, columns]
         return pltpu.make_async_remote_copy(
-            src_ref=source,
+            src_ref=grids[step].at[1 + plane, columns],
             dst_ref=grids[step].at[halo, columns],
             send_sem=x_send.at[step, way, q],
             recv_sem=x_recv.at[step, way, q],
@@ -145,11 +151,13 @@
                 for one in copies:
                     one.wait_recv()
 
+    for q in range(Q):
+        for way in (0, 1):
+            face_load(way, q).wait()
+            start("rows", way, [x_copy(0, way, q)])
     for way in (0, 1):
         start("cols", way, [z_copy(0, way, part) for part in range(3)])
-    for q in range(Q):
-        for way in (0, 1):
-            start("rows", way, [x_copy(0, way, q)])
+    load_field.start()
     load_cells.start()
 
     zero = jnp.zeros((K, L), jnp.float32)
@@ -305,8 +313,9 @@
 
 def sum_kernel(scale, field, below, potential, field_end, sums, end_sem, sum_sem):
     J, I = field.shape[0], field.shape[1]
-    Q = pieces_of(I)
+    Q = pieces_of(I, (4, 2))
     W = I // Q
+
     whole = pltpu.make_async_copy(field, field_end, end_sem)
     whole.start()
 
@@ -337,7 +346,7 @@
 
     def on_device(field_values, crowding):
         J, I, K, L = field_values.shape
-        Q = pieces_of(I)
+        Q = pieces_of(I, (2,))
         padded = pltpu.VMEM((J + 2, I + 2, K, L), jnp.float32)
         block = jax.ShapeDtypeStruct((J, I, K, L), jnp.float32)
         vector = pl.BlockSpec(memory_space=pltpu.VMEM)
@@ -369,6 +378,7 @@
                 dma((Q,)),
                 dma((Q,)),
                 dma((2,)),
+                dma((2, Q)),
             ],
             compiler_params=pltpu.CompilerParams(
                 collective_id=0,
@@ -382,7 +392,7 @@
             out_shape=(block, block),
             in_specs=[vector, vector],
             out_specs=(anywhere, anywhere),
-            scratch_shapes=[pltpu.VMEM((J, I, K, L), jnp.float32), dma, dma((Q,))],
+            scratch_shapes=[pltpu.VMEM((J, I, K, L), jnp.float32), dma, dma((pieces_of(I, (4, 2)),))],
             compiler_params=pltpu.CompilerParams(vmem_limit_bytes=16 * 1024 * 1024),
         )(field_end, below)
         return potential, field_end

time: 53.3 us -> 52.9 us (level)
  no operation moved by 1% of the time
where the time goes in v3:
time: 52.9 us; the launch traced here: 52.7 us
  Pallas kernels  52.1 us (98%)
  between operations  0.64 us (1%)
    pallas_call x1, Pallas kernels, on_device(): pl.pallas_call(functools.partial(march_kernel, sizes), out_shape=(pltpu.V...  48.8 us
    pallas_call x1, Pallas kernels, on_device(): pl.pallas_call(functools.partial(sum_kernel, 1.0 / (J * sizes['rows'])),...  3.34 us

profile of v3, /device:TPU:0, one launch (start us, length us, event | category | flops | bytes accessed | tf_op | source)
XLA Modules:
  0.0 52.7 jit_solution(2337793874574652345)
XLA Ops:
  0.6 48.8 %shard_map.41 = (f32[8,16,64,128]{3,2,1,0:T(8,128)S(1)}, f32[16,64,128]{2,1,0:T(8,128)S(1)}) custom-call(f32[8,16,64,128]{3,2,1,0:T(8,128)} %field.1, f32[8,16,64,128]{3,2,1,0:T(8,128)} %crowd.1), custom_call_target="tpu_custom_call" | custom-call | tf_op jit(solution)/shard_map/pallas_call | solution.py:355
  49.4 3.3 %shard_map.42 = (f32[8,16,64,128]{3,2,1,0:T(8,128)}, f32[8,16,64,128]{3,2,1,0:T(8,128)}) custom-call(f32[8,16,64,128]{3,2,1,0:T(8,128)S(1)} %get-tuple-element.4.field, f32[16,64,128]{2,1,0:T(8,128)S(1)} %get-tuple-element.5.below), custom_call_target="tpu_custom_call" | custom-call | tf_op jit(solution)/shard_map/pallas_call | solution.py:390
